TPU v7x, 32 devices: a whole 2x2x4 slice. The times are simulated.
32 devices in a mesh: samples: 2 (over x), px: 8 (over z, y), py: 2 (over core).
Axes of the slice: x: 2, y: 2, z: 4, core: 2. Of those that a mesh axis runs over, the one named last changes fastest.
Arguments:
- source: float32 [2, 512, 256, 256], P(None, 'samples', 'px', 'py'), parts along dimension 1, may hold values from -6 to 6
- speed: float32 [512, 256, 256], P('samples', 'px', 'py'), parts along dimension 0, may hold values from 0.5 to 3
Outputs:
- solution: float32 [2, 512, 256, 256], P(None, 'samples', 'px', 'py'), parts along dimension 1
There are 2 independent parts, one for each index of `samples`. A program takes and returns all parts, laid end to end along the dimension named above; each array names one. Nothing has to cross between parts.
All inputs are finite; a program needn't handle non-finite values.
Results may differ from a plain program's by a relative error of at most 0.00024.
Values sent between devices are 32-bit elements; how exact they have to be, the bound alone decides.
A program may use at most 192 MiB of HBM per device.

v0:
```python
import functools

import jax
import jax.numpy as jnp
import numpy as np
from jax import lax
from jax.experimental import pallas as pl
from jax.experimental.pallas import tpu as pltpu
from jax.sharding import PartitionSpec as P

wave_square = 0.25
damped = 0.125
epsilon = 1e-06
rows = 8
lanes = 128
MESH = pl.DeviceIdType.MESH


def sine_table(length):
    index = np.arange(length, dtype=np.int64) + 1
    turns = (index[:, None] * index[None, :]) % (2 * (length + 1))
    table = np.sqrt(2.0 / (length + 1.0)) * np.sin(np.pi * turns / (length + 1.0))
    high = table.astype(np.float32).astype(jnp.bfloat16)
    low = (table - high.astype(np.float64)).astype(np.float32).astype(jnp.bfloat16)
    return jnp.asarray(high), jnp.asarray(low)


def eigen_line(length):
    sine_half = np.sin(np.pi * (np.arange(length) + 1.0) / (2.0 * (length + 1.0)))
    return 4.0 * sine_half * sine_half


def root_table(length_x, length_z):
    half = eigen_line(length_x)[:, None] + eigen_line(length_z)[None, :]
    half = (half + 2.0 - wave_square + 1j * damped) / 2.0
    root = 1.0 / (half + np.sqrt(half * half - 1.0))
    return jnp.asarray(np.stack([root.real, root.imag]).astype(np.float32))


def halves(values):
    high = values.astype(jnp.bfloat16)
    low = (values - high.astype(jnp.float32)).astype(jnp.bfloat16)
    return high, low


def dot_three(left, right):
    dot = functools.partial(jnp.dot, preferred_element_type=jnp.float32)
    return dot(left[0], right[0]) + (dot(left[0], right[1]) + dot(left[1], right[0]))


def times(a, b):
    return a[0] * b[0] - a[1] * b[1], a[0] * b[1] + a[1] * b[0]


def plus(a, b):
    return a[0] + b[0], a[1] + b[1]


def inverse(a):
    scale = 1.0 / (a[0] * a[0] + a[1] * a[1])
    return a[0] * scale, -a[1] * scale


def minus(a, b):
    return a[0] - b[0], a[1] - b[1]


def power(a, number):
    result = None
    while number:
        if number & 1:
            result = a if result is None else times(result, a)
        number >>= 1
        if number:
            a = times(a, a)
    return result


def pair_of(ref, plane=0):
    return ref[plane], ref[plane + 1]


def greet(peers):
    barrier = pltpu.get_barrier_semaphore()
    for peer in peers:
        pl.semaphore_signal(barrier, inc=1, device_id=peer, device_id_type=MESH)
    pl.semaphore_wait(barrier, len(peers))


def remote(source, target, sends, receives, place, device):
    return pltpu.make_async_remote_copy(
        src_ref=source,
        dst_ref=target,
        send_sem=sends.at[place],
        recv_sem=receives.at[place],
        device_id=device,
        device_id_type=MESH,
    )


def solve_all(
    blocks,
    parts,
    source_ref,
    speed_ref,
    roots_ref,
    x_high_ref,
    x_low_ref,
    z_high_ref,
    z_low_ref,
    image,
    total_ref,
    source,
    speed,
    roots,
    jumps,
    tiles,
    modes,
    ends,
    pair,
    pairs,
    answer,
    carry,
    inner,
    edges,
    slots,
    x_halves,
    z_halves,
    sums_ref,
    heard,
    source_sem,
    speed_sem,
    table_sem,
    in_send,
    in_recv,
    ends_send,
    ends_recv,
    pair_send,
    pair_recv,
    carry_send,
    carry_recv,
    edge_send,
    edge_recv,
    out_send,
    out_recv,
    sum_send,
    sum_recv,
):
    steps, _, _, number, tile, _ = tiles.shape
    _, length, _, _ = source.shape
    bands = number // rows
    part = length // parts
    length_z = modes.shape[-1]
    groups, _, _, span, _ = ends.shape
    per, places = span // tile, blocks // 2
    me = lax.axis_index("px")
    side, place = lax.rem(me, 2), lax.div(me, 2)
    other = me + 1 - 2 * side
    mine = lax.axis_index("py")
    beside = {"py": 1 - mine}
    others = [lax.rem(place + k, places) for k in range(1, places)]
    everyone = []
    for k in range(1, blocks * parts):
        peer = lax.rem(me * parts + mine + k, blocks * parts)
        everyone.append({"px": lax.div(peer, parts), "py": lax.rem(peer, parts)})

    def band(y):
        return pl.ds(pl.multiple_of(y * rows, rows), rows)

    def load_source(i):
        return pltpu.make_async_copy(
            source_ref.at[lax.div(i, bands), :, band(lax.rem(i, bands))], source.at[i], source_sem.at[i]
        )

    def load_speed(y):
        return pltpu.make_async_copy(speed_ref.at[:, band(y)], speed.at[y], speed_sem.at[y])

    root_rows = pl.ds(pl.multiple_of(mine * part, 8), part)
    tables = [
        (x_high_ref, x_halves.at[0]),
        (x_low_ref, x_halves.at[1]),
        (z_high_ref, z_halves.at[0]),
        (z_low_ref, z_halves.at[1]),
        (roots_ref.at[:, root_rows], roots),
    ]
    tables = [pltpu.make_async_copy(a, b, table_sem.at[k]) for k, (a, b) in enumerate(tables)]
    load_source(0).start()
    for copy in tables:
        copy.start()

    @pl.loop(1, 2 * bands)
    def _(i):
        load_source(i).start()

    @pl.loop(0, bands)
    def _(y):
        load_speed(y).start()

    greet(everyone)
    for copy in tables[:2]:
        copy.wait()
    x_table = (x_halves[0], x_halves[1])

    def slot_of(h, own):
        return own + lax.rem(h + own, 2) * (2 - own)

    def send_in(i):
        c, y = lax.div(i, bands), lax.rem(i, bands)
        return remote(
            tiles.at[:, 2, c, band(y)], tiles.at[:, mine, c, band(y)], in_send, in_recv, i, beside
        )

    @pl.loop(0, 2 * bands)
    def _(i):
        load_source(i).wait()
        c, y = lax.div(i, bands), lax.rem(i, bands)
        flat = source.at[i].reshape(length * rows, lanes)
        for j in range(0, rows, 2):
            pieces = [flat[pl.ds(j + k, length, stride=rows), :] for k in range(2)]
            result = dot_three(x_table, halves(jnp.concatenate(pieces, axis=1)))
            for k in range(2):
                for h in range(parts):
                    block = result[h * part : (h + 1) * part, k * lanes : (k + 1) * lanes]
                    tiles[:, slot_of(h, mine), c, y * rows + j + k] = block.reshape(steps, tile, lanes)
        send_in(i).start()

    for copy in tables[2:]:
        copy.wait()
    table = (z_halves[0], z_halves[1])
    zero = jnp.zeros((tile, length_z), jnp.float32)
    own_lanes = pl.ds(pl.multiple_of(side * lanes, lanes), lanes)
    jump = power((roots[0, :, own_lanes], roots[1, :, own_lanes]), number)
    jumps[0] = jump[0]
    jumps[1] = jump[1]

    def send_ends(k, i):
        spot = pl.ds(pl.multiple_of(i * tile, tile), tile)
        return remote(
            ends.at[k, 2, :, spot],
            ends.at[k, side, :, spot],
            ends_send,
            ends_recv,
            k * per + i,
            {"px": other},
        )

    def send_pair(k):
        return [
            remote(
                pair.at[k, :, pl.ds(pl.multiple_of(peer * rows, rows), rows)],
                pairs.at[k, place],
                pair_send.at[k],
                pair_recv.at[k],
                i,
                {"px": 2 * peer + side},
            )
            for i, peer in enumerate(others)
        ]

    def send_carry(k):
        return [
            remote(
                answer.at[k, peer],
                carry.at[k, :, pl.ds(pl.multiple_of(place * rows, rows), rows)],
                carry_send.at[k],
                carry_recv.at[k],
                i,
                {"px": 2 * peer + side},
            )
            for i, peer in enumerate(others)
        ]

    def send_edges(k):
        return remote(inner.at[k, 1 - side], edges.at[k, side], edge_send, edge_recv, k, {"px": other})

    def group_jump(k):
        part = pl.ds(k * span, span) if isinstance(k, int) else pl.ds(pl.multiple_of(k * span, span), span)
        return jumps[0, part], jumps[1, part]

    def tile_root(i):
        part = pl.ds(pl.multiple_of(i * tile, tile), tile)
        return roots[0, part], roots[1, part]

    def forward(k, i):
        s = k * per + i
        for c in range(2):
            pieces = [tiles[s, h, c].reshape(number * tile, lanes) for h in range(parts)]
            result = dot_three(halves(jnp.concatenate(pieces, axis=1)), table)
            modes[s, c] = result.reshape(number, tile, length_z)
        root = tile_root(s)

        def step(j, state):
            first, last = state
            back = number - 1 - j
            last = plus(times(root, last), (modes[s, 0, j], modes[s, 1, j]))
            first = plus(times(root, first), (modes[s, 0, back], modes[s, 1, back]))
            return first, last

        first, last = lax.fori_loop(0, number, step, ((zero, zero), (zero, zero)), unroll=4)
        part = pl.ds(pl.multiple_of(i * tile, tile), tile)
        for h in range(2):
            slot = slot_of(h, side)
            for plane, value in enumerate(first + last):
                ends[k, slot, plane, part] = value[:, h * lanes : (h + 1) * lanes]
        send_ends(k, i).start()

    def merge(k):
        for i in range(per):
            send_ends(k, i).wait_recv()
        rate = group_jump(k)
        first = plus(pair_of(ends.at[k, 0]), times(rate, pair_of(ends.at[k, 1])))
        last = plus(pair_of(ends.at[k, 1], 2), times(rate, pair_of(ends.at[k, 0], 2)))
        for plane, value in enumerate(first + last):
            pair[k, plane] = value
        own = pl.ds(pl.multiple_of(place * rows, rows), rows)
        pairs[k, place] = pair[k, :, own]
        for copy in send_pair(k):
            copy.start()

    def solve(k):
        for copy in send_pair(k):
            copy.wait_recv()
        own = pl.ds(pl.multiple_of(k * span + place * rows, rows), rows)
        root = (roots[0, own, own_lanes], roots[1, own, own_lanes])
        rate = (jumps[0, own], jumps[1, own])
        rate = times(rate, rate)
        whole = power(root, blocks * number + 1)
        square = times(whole, whole)
        spread = inverse((1.0 - square[0], -square[1]))
        spread = times((-root[0], -root[1]), spread)
        none = jnp.zeros((rows, lanes), jnp.float32)
        from_left, from_right = (none, none), (none, none)
        for q in range(places):
            from_left = plus(pair_of(pairs.at[k, q], 2), times(rate, from_left))
            from_right = plus(pair_of(pairs.at[k, places - 1 - q]), times(rate, from_right))
        before = times(spread, minus(from_right, times(whole, from_left)))
        after = times(spread, minus(from_left, times(whole, from_right)))
        for q in range(places):
            p = places - 1 - q
            for c in range(2):
                answer[k, q, c] = before[c]
                answer[k, p, 2 + c] = after[c]
            before = plus(pair_of(pairs.at[k, q], 2), times(rate, before))
            after = plus(pair_of(pairs.at[k, p]), times(rate, after))
        mine_rows = pl.ds(pl.multiple_of(place * rows, rows), rows)
        carry[k, :, mine_rows] = answer[k, place]
        for copy in send_carry(k):
            copy.start()

    def expand(k):
        for copy in send_carry(k):
            copy.wait_recv()
        rate = group_jump(k)
        before, after = pair_of(carry.at[k]), pair_of(carry.at[k], 2)
        left = before + plus(pair_of(ends.at[k, 1]), times(rate, after))
        right = plus(pair_of(ends.at[k, 0], 2), times(rate, before)) + after
        for q, values in enumerate((left, right)):
            for plane, value in enumerate(values):
                inner[k, q, plane] = value
        send_edges(k).start()
        edges[k, side] = inner[k, side]

    def send_out(i):
        spot = pl.ds(pl.multiple_of(i * tile, tile), tile)
        return remote(slots.at[2, :, :, spot], slots.at[mine, :, :, spot], out_send, out_recv, i, beside)

    wide = 2 if per % 2 == 0 else 1

    def backward(k, i):
        spots = [i * wide + n for n in range(wide)]
        tiles_here = [k * per + spot for spot in spots]
        own = [tile_root(s) for s in tiles_here]

        def side_of(plane):
            return [
                tuple(
                    jnp.concatenate(
                        [
                            edges[k, h, plane + c, pl.ds(pl.multiple_of(spot * tile, tile), tile)]
                            for h in range(2)
                        ],
                        axis=1,
                    )
                    for c in range(2)
                )
                for spot in spots
            ]

        before, after = side_of(0), side_of(2)

        def mode(s, j):
            return modes[s, 0, j], modes[s, 1, j]

        def keep(s, j, value):
            modes[s, 0, j] = value[0]
            modes[s, 1, j] = value[1]

        def ahead(j, states):
            states = [plus(times(r, v), mode(s, j)) for s, r, v in zip(tiles_here, own, states)]
            for s, value in zip(tiles_here, states):
                keep(s, j, value)
            return states

        lasts = lax.fori_loop(0, number, ahead, before, unroll=2)
        values = []
        for root, last, far in zip(own, lasts, after):
            square = times(root, root)
            scaled = times(root, inverse((1.0 - square[0], -square[1])))
            values.append(times(scaled, plus(times(root, last), far)))

        def back(j, values):
            j = number - 1 - j
            values = [times(r, plus(v, mode(s, j))) for s, r, v in zip(tiles_here, own, values)]
            for s, value in zip(tiles_here, values):
                keep(s, j, value)
            return values

        lax.fori_loop(0, number, back, values, unroll=2)

        @pl.loop(0, wide)
        def _(n):
            s = k * per + i * wide + n
            for c in range(2):
                result = dot_three(halves(modes[s, c].reshape(number * tile, length_z)), table)
                spot = pl.ds(pl.multiple_of(s * tile, tile), tile)
                for h in range(parts):
                    block = result[:, h * lanes : (h + 1) * lanes]
                    slots[slot_of(h, mine), c, :, spot] = block.reshape(number, tile, lanes)
            send_out(s).start()

    @pl.loop(0, 2 * bands)
    def _(i):
        send_in(i).wait_recv()

    lag = 2

    @pl.loop(0, groups)
    def _(k):
        @pl.loop(0, per)
        def _(i):
            forward(k, i)

        @pl.when(k >= lag)
        def _():
            merge(k - lag)

    early = 3
    stages = [(k, 3.4, merge, k) for k in range(max(groups - lag, 0), groups)]
    stages += [(k, 6.7, solve, k) for k in range(groups)]
    stages += [(k, 10.0, expand, k) for k in range(min(early, groups))]
    for _, _, stage, k in sorted(stages, key=lambda item: 1.8 * item[0] + item[1]):
        stage(k)

    @pl.loop(0, groups)
    def _(k):
        send_edges(k).wait_recv()

        @pl.loop(0, per // wide)
        def _(i):
            backward(k, i)

        @pl.when(k + early < groups)
        def _():
            expand(k + early)

    @pl.loop(0, groups)
    def _(k):
        send_edges(k).wait_send()
        for copy in [send_ends(k, i) for i in range(per)] + send_pair(k) + send_carry(k):
            copy.wait_send()

    @pl.loop(0, 2 * bands)
    def _(i):
        send_in(i).wait_send()

    @pl.loop(0, steps)
    def _(i):
        send_out(i).wait_recv()

    sums_ref[...] = jnp.zeros_like(sums_ref)
    group = 8

    @pl.loop(0, bands)
    def _(y):
        load_speed(y).wait()
        flat = image.at[y].reshape(2 * length * rows, lanes)
        for c in range(2):
            for j in range(0, rows, 2):
                pieces = [
                    jnp.concatenate([slots[h, c, y * rows + j + k] for h in range(parts)], axis=0)
                    for k in range(2)
                ]
                result = dot_three(x_table, halves(jnp.concatenate(pieces, axis=1)))
                for k in range(2):
                    flat[pl.ds(c * length * rows + j + k, length, stride=rows), :] = result[
                        :, k * lanes : (k + 1) * lanes
                    ]

        def step(i, sums):
            some = pl.ds(i * group, group)
            v = speed[y, some]
            shift = wave_square - wave_square / (v * v)
            s_re, s_im = source[y, some], source[bands + y, some]
            w_re, w_im = image[y, 0, some], image[y, 1, some]
            u_re = s_re + shift * w_re + damped * w_im
            u_im = s_im + shift * w_im - damped * w_re
            terms = (
                s_re * s_re + s_im * s_im,
                s_re * u_re + s_im * u_im,
                s_re * u_im - s_im * u_re,
                u_re * u_re + u_im * u_im,
            )
            return tuple(a + jnp.sum(b, axis=0) for a, b in zip(sums, terms))

        none = jnp.zeros((rows, lanes), jnp.float32)
        sums = lax.fori_loop(0, length // group, step, (none,) * 4)
        for k in range(4):
            sums_ref[pl.ds(k, 1)] += jnp.sum(sums[k], axis=0, keepdims=True)

    copies = [
        remote(sums_ref, heard.at[k], sum_send, sum_recv, k, peer) for k, peer in enumerate(everyone)
    ]
    for copy in copies:
        copy.start()
    for copy in copies:
        copy.wait()
    total_ref[...] = sums_ref[...] + jnp.sum(heard[...], axis=0)

    @pl.loop(0, steps)
    def _(i):
        send_out(i).wait_send()


def scale(total_ref, w_ref, out_ref):
    sums = jnp.sum(total_ref[...], axis=1, keepdims=True)
    size = sums[0:1] + epsilon
    one_re, one_im, squares = sums[1:2] / size, sums[2:3] / size, sums[3:4] / size
    one = one_re * one_re + one_im * one_im
    denominator = squares - one * (epsilon / size) + epsilon
    re = jnp.broadcast_to(one_re / denominator, (rows, lanes))
    im = jnp.broadcast_to(-one_im / denominator, (rows, lanes))
    bands, depth = w_ref.shape[0], out_ref.shape[1]
    base = pl.program_id(0) * depth

    @pl.loop(0, depth, unroll=4)
    def _(x):
        for y in range(bands):
            w_re, w_im = w_ref[y, 0, base + x], w_ref[y, 1, base + x]
            out_ref[0, x, y * rows : (y + 1) * rows] = re * w_re - im * w_im
            out_ref[1, x, y * rows : (y + 1) * rows] = re * w_im + im * w_re


def on_device(blocks, parts, source, speed):
    _, length_x, number, width = source.shape
    length_z = width * parts
    part = length_x // parts
    tile = 2 * rows
    bands, tiles = number // rows, part // tile
    span = rows * blocks // 2
    groups, places, peers = part // span, blocks // 2, blocks * parts - 1
    f32 = jnp.float32
    shape, dma = jax.ShapeDtypeStruct, pltpu.SemaphoreType.DMA

    def vmem(*size):
        return pltpu.VMEM(size, f32)

    anywhere, inside = pl.BlockSpec(memory_space=pl.ANY), pl.BlockSpec(memory_space=pltpu.VMEM)
    image, sums = pl.pallas_call(
        functools.partial(solve_all, blocks, parts),
        in_specs=[anywhere] * 7,
        out_specs=[inside, inside],
        out_shape=[vmem(bands, 2, length_x, rows, width), vmem(rows, width)],
        scratch_shapes=[
            vmem(2 * bands, length_x, rows, width),
            vmem(bands, length_x, rows, width),
            vmem(2, part, length_z),
            vmem(2, part, lanes),
            vmem(tiles, 3, 2, number, tile, width),
            vmem(tiles, 2, number, tile, length_z),
            vmem(groups, 3, 4, span, lanes),
            vmem(groups, 4, span, lanes),
            vmem(groups, places, 4, rows, lanes),
            vmem(groups, places, 4, rows, lanes),
            vmem(groups, 4, span, lanes),
            vmem(groups, 2, 4, span, lanes),
            vmem(groups, 2, 4, span, lanes),
            vmem(3, 2, number, part, width),
            pltpu.VMEM((2, length_x, length_x), jnp.bfloat16),
            pltpu.VMEM((2, length_z, length_z), jnp.bfloat16),
            vmem(rows, width),
            vmem(peers, rows, width),
            dma((2 * bands,)),
            dma((bands,)),
            dma((5,)),
            dma((2 * bands,)),
            dma((2 * bands,)),
        ]
        + [dma((tiles,))] * 2
        + [dma((groups, places - 1))] * 4
        + [dma((groups,))] * 2
        + [dma((tiles,))] * 2
        + [dma((peers,))] * 2,
        compiler_params=pltpu.CompilerParams(
            vmem_limit_bytes=55 * 1024 * 1024, collective_id=0, has_side_effects=True
        ),
        name="solve_all",
    )(source, speed, root_table(length_x, length_z), *sine_table(length_x), *sine_table(length_z))
    pieces = 8
    return pl.pallas_call(
        scale,
        grid=(pieces,),
        in_specs=[inside, inside],
        out_specs=pl.BlockSpec((2, length_x // pieces, number, width), lambda i: (0, i, 0, 0)),
        out_shape=shape(source.shape, f32),
        compiler_params=pltpu.CompilerParams(
            dimension_semantics=("arbitrary",), vmem_limit_bytes=16 * 1024 * 1024
        ),
        name="scale",
    )(sums, image)


def solution(mesh):
    return jax.shard_map(
        functools.partial(on_device, mesh.shape["px"], mesh.shape["py"]),
        mesh=mesh,
        in_specs=(P(None, "samples", "px", "py"), P("samples", "px", "py")),
        out_specs=P(None, "samples", "px", "py"),
        check_vma=False,
    )
```

profile of v0, /device:TPU:0, one launch (start us, length us, event | category | flops | bytes accessed | tf_op | source)
XLA Modules:
  0.0 62.8 jit_solution(17462458668233596916)
XLA Ops:
  0.0 57.5 %solve_all.1 = (f32[4,2,256,8,128]{4,3,2,1,0:T(8,128)S(1)}, f32[8,128]{1,0:T(8,128)S(1)}) custom-call(f32[2,256,32,128]{3,2,1,0:T(8,128)} %source_ref.1, f32[256,32,128]{2,1,0:T(8,128)} %speed_ref.1, f32[2,256,256]{2,1,0:T(8,128)} %constant.6.clone.roots_ref, bf16[256,256]{1,0:T(8,128)(2,1)} %constant.7.clone.x_high_ref.z_high_ref, ...), custom_call_target="tpu_custom_call" | custom-call | tf_op jit(solution)/shard_map/solve_all/pallas_call | solution.py:568
  57.5 5.4 %scale.1 = f32[2,256,32,128]{3,2,1,0:T(8,128)} custom-call(f32[8,128]{1,0:T(8,128)S(1)} %get-tuple-element.7.total_ref, f32[4,2,256,8,128]{4,3,2,1,0:T(8,128)S(1)} %get-tuple-element.8.w_ref), custom_call_target="tpu_custom_call" | custom-call | tf_op jit(solution)/shard_map/scale/pallas_call | solution.py:609
where the time goes:
time: 63 us; the launch traced here: 62.8 us
  Pallas kernels  62.8 us (100%)
    pallas_call x1, Pallas kernels, on_device(): pl.pallas_call(functools.partial(solve_all, blocks, parts), in_specs=[any...  57.5 us
    pallas_call x1, Pallas kernels, on_device(): pl.pallas_call(scale, grid=(pieces,), in_specs=[inside, inside], out_spec...  5.37 us

commit v1 on v0

--- a/solution.py
+++ b/solution.py
@@ -113,14 +113,13 @@
     source,
     speed,
     roots,
-    jumps,
+    rates,
     tiles,
     modes,
     ends,
     pair,
-    pairs,
-    answer,
-    carry,
+    waves_out,
+    waves,
     inner,
     edges,
     slots,
@@ -135,10 +134,8 @@
     in_recv,
     ends_send,
     ends_recv,
-    pair_send,
-    pair_recv,
-    carry_send,
-    carry_recv,
+    wave_send,
+    wave_recv,
     edge_send,
     edge_recv,
     out_send,
@@ -158,7 +155,11 @@
     other = me + 1 - 2 * side
     mine = lax.axis_index("py")
     beside = {"py": 1 - mine}
-    others = [lax.rem(place + k, places) for k in range(1, places)]
+    depths = places // 2
+    behind = lax.div(place, depths)
+    depth = place + behind * (places - 1 - 2 * place)
+    inmost = lax.div(depth + 1, depths)
+    toward = 1 - 2 * behind
     everyone = []
     for k in range(1, blocks * parts):
         peer = lax.rem(me * parts + mine + k, blocks * parts)
@@ -229,9 +230,20 @@
     table = (z_halves[0], z_halves[1])
     zero = jnp.zeros((tile, length_z), jnp.float32)
     own_lanes = pl.ds(pl.multiple_of(side * lanes, lanes), lanes)
-    jump = power((roots[0, :, own_lanes], roots[1, :, own_lanes]), number)
-    jumps[0] = jump[0]
-    jumps[1] = jump[1]
+    root = (roots[0, :, own_lanes], roots[1, :, own_lanes])
+    jump = power(root, number)
+    rate = times(jump, jump)
+    double = times(rate, rate)
+    echo = (-root[0], -root[1])
+    for n in range(1, depths):
+        deeper = times(echo, double)
+        echo = tuple(jnp.where(depth >= n, a, b) for a, b in zip(deeper, echo))
+    whole = power(root, blocks * number + 1)
+    square = times(whole, whole)
+    spread = inverse((1.0 - square[0], -square[1]))
+    for n, values in enumerate((jump, rate, echo, whole, spread)):
+        rates[2 * n] = values[0]
+        rates[2 * n + 1] = values[1]
 
     def send_ends(k, i):
         spot = pl.ds(pl.multiple_of(i * tile, tile), tile)
@@ -244,38 +256,28 @@
             {"px": other},
         )
 
-    def send_pair(k):
-        return [
-            remote(
-                pair.at[k, :, pl.ds(pl.multiple_of(peer * rows, rows), rows)],
-                pairs.at[k, place],
-                pair_send.at[k],
-                pair_recv.at[k],
-                i,
-                {"px": 2 * peer + side},
-            )
-            for i, peer in enumerate(others)
-        ]
-
-    def send_carry(k):
-        return [
-            remote(
-                answer.at[k, peer],
-                carry.at[k, :, pl.ds(pl.multiple_of(place * rows, rows), rows)],
-                carry_send.at[k],
-                carry_recv.at[k],
-                i,
-                {"px": 2 * peer + side},
-            )
-            for i, peer in enumerate(others)
-        ]
+    def wave(k, way, slot, place):
+        return pltpu.make_async_remote_copy(
+            src_ref=waves_out.at[k, way],
+            dst_ref=waves.at[k, slot],
+            send_sem=wave_send.at[2 * k + way],
+            recv_sem=wave_recv.at[2 * k + slot],
+            device_id={"px": 2 * place + side},
+            device_id_type=MESH,
+        )
+
+    def send_inward(k):
+        return wave(k, 0, inmost, place + toward)
+
+    def send_outward(k):
+        return wave(k, 1, 1, place - toward)
 
     def send_edges(k):
         return remote(inner.at[k, 1 - side], edges.at[k, side], edge_send, edge_recv, k, {"px": other})
 
-    def group_jump(k):
+    def group_rates(k, *which):
         part = pl.ds(k * span, span) if isinstance(k, int) else pl.ds(pl.multiple_of(k * span, span), span)
-        return jumps[0, part], jumps[1, part]
+        return [(rates[2 * n, part], rates[2 * n + 1, part]) for n in which]
 
     def tile_root(i):
         part = pl.ds(pl.multiple_of(i * tile, tile), tile)
@@ -304,56 +306,57 @@
                 ends[k, slot, plane, part] = value[:, h * lanes : (h + 1) * lanes]
         send_ends(k, i).start()
 
+    def either(a, b):
+        return tuple(jnp.where(behind == 0, x, y) for x, y in zip(a, b))
+
+    def pass_inward(k, rate, echo, came):
+        bounced = times(echo, pair_of(pair.at[k], 2))
+        value = plus(pair_of(pair.at[k]), times(rate, plus(came, bounced)))
+        for c in range(2):
+            waves_out[k, 0, c] = value[c]
+        send_inward(k).start()
+
     def merge(k):
         for i in range(per):
             send_ends(k, i).wait_recv()
-        rate = group_jump(k)
-        first = plus(pair_of(ends.at[k, 0]), times(rate, pair_of(ends.at[k, 1])))
-        last = plus(pair_of(ends.at[k, 1], 2), times(rate, pair_of(ends.at[k, 0], 2)))
-        for plane, value in enumerate(first + last):
+        jump, rate, echo = group_rates(k, 0, 1, 2)
+        first = plus(pair_of(ends.at[k, 0]), times(jump, pair_of(ends.at[k, 1])))
+        last = plus(pair_of(ends.at[k, 1], 2), times(jump, pair_of(ends.at[k, 0], 2)))
+        for plane, value in enumerate(either(last, first) + either(first, last)):
             pair[k, plane] = value
-        own = pl.ds(pl.multiple_of(place * rows, rows), rows)
-        pairs[k, place] = pair[k, :, own]
-        for copy in send_pair(k):
-            copy.start()
-
-    def solve(k):
-        for copy in send_pair(k):
-            copy.wait_recv()
-        own = pl.ds(pl.multiple_of(k * span + place * rows, rows), rows)
-        root = (roots[0, own, own_lanes], roots[1, own, own_lanes])
-        rate = (jumps[0, own], jumps[1, own])
-        rate = times(rate, rate)
-        whole = power(root, blocks * number + 1)
-        square = times(whole, whole)
-        spread = inverse((1.0 - square[0], -square[1]))
-        spread = times((-root[0], -root[1]), spread)
-        none = jnp.zeros((rows, lanes), jnp.float32)
-        from_left, from_right = (none, none), (none, none)
-        for q in range(places):
-            from_left = plus(pair_of(pairs.at[k, q], 2), times(rate, from_left))
-            from_right = plus(pair_of(pairs.at[k, places - 1 - q]), times(rate, from_right))
-        before = times(spread, minus(from_right, times(whole, from_left)))
-        after = times(spread, minus(from_left, times(whole, from_right)))
-        for q in range(places):
-            p = places - 1 - q
+
+        @pl.when(depth == 0)
+        def _():
+            none = jnp.zeros((span, lanes), jnp.float32)
             for c in range(2):
-                answer[k, q, c] = before[c]
-                answer[k, p, 2 + c] = after[c]
-            before = plus(pair_of(pairs.at[k, q], 2), times(rate, before))
-            after = plus(pair_of(pairs.at[k, p]), times(rate, after))
-        mine_rows = pl.ds(pl.multiple_of(place * rows, rows), rows)
-        carry[k, :, mine_rows] = answer[k, place]
-        for copy in send_carry(k):
-            copy.start()
+                waves[k, 0, c] = none
+            pass_inward(k, rate, echo, (none, none))
+
+    def relay(k):
+        @pl.when(depth > 0)
+        def _():
+            wave(k, 0, 0, place - toward).wait_recv()
+            rate, echo = group_rates(k, 1, 2)
+            pass_inward(k, rate, echo, pair_of(waves.at[k, 0]))
 
     def expand(k):
-        for copy in send_carry(k):
-            copy.wait_recv()
-        rate = group_jump(k)
-        before, after = pair_of(carry.at[k]), pair_of(carry.at[k], 2)
-        left = before + plus(pair_of(ends.at[k, 1]), times(rate, after))
-        right = plus(pair_of(ends.at[k, 0], 2), times(rate, before)) + after
+        wave(k, 1, 1, place + toward).wait_recv()
+        jump, rate, echo, whole, spread = group_rates(k, 0, 1, 2, 3, 4)
+        came = pair_of(waves.at[k, 1])
+        met = times(spread, minus(came, times(whole, pair_of(waves_out.at[k, 0]))))
+        came = tuple(jnp.where(inmost == 1, a, b) for a, b in zip(met, came))
+        out = plus(pair_of(pair.at[k], 2), times(rate, came))
+        back = plus(pair_of(waves.at[k, 0]), times(echo, out))
+
+        @pl.when(depth > 0)
+        def _():
+            for c in range(2):
+                waves_out[k, 1, c] = out[c]
+            send_outward(k).start()
+
+        before, after = either(back, came), either(came, back)
+        left = before + plus(pair_of(ends.at[k, 1]), times(jump, after))
+        right = plus(pair_of(ends.at[k, 0], 2), times(jump, before)) + after
         for q, values in enumerate((left, right)):
             for plane, value in enumerate(values):
                 inner[k, q, plane] = value
@@ -445,10 +448,10 @@
             merge(k - lag)
 
     early = 3
-    stages = [(k, 3.4, merge, k) for k in range(max(groups - lag, 0), groups)]
-    stages += [(k, 6.7, solve, k) for k in range(groups)]
-    stages += [(k, 10.0, expand, k) for k in range(min(early, groups))]
-    for _, _, stage, k in sorted(stages, key=lambda item: 1.8 * item[0] + item[1]):
+    stages = [(2.9, merge, k) for k in range(max(groups - lag, 0), groups)]
+    stages += [(5.2, relay, k) for k in range(groups)]
+    stages += [(8.7, expand, k) for k in range(min(early, groups))]
+    for _, stage, k in sorted(stages, key=lambda item: 1.8 * item[2] + item[0]):
         stage(k)
 
     @pl.loop(0, groups)
@@ -466,8 +469,13 @@
     @pl.loop(0, groups)
     def _(k):
         send_edges(k).wait_send()
-        for copy in [send_ends(k, i) for i in range(per)] + send_pair(k) + send_carry(k):
-            copy.wait_send()
+        send_inward(k).wait_send()
+        for i in range(per):
+            send_ends(k, i).wait_send()
+
+        @pl.when(depth > 0)
+        def _():
+            send_outward(k).wait_send()
 
     @pl.loop(0, 2 * bands)
     def _(i):
@@ -557,7 +565,7 @@
     tile = 2 * rows
     bands, tiles = number // rows, part // tile
     span = rows * blocks // 2
-    groups, places, peers = part // span, blocks // 2, blocks * parts - 1
+    groups, peers = part // span, blocks * parts - 1
     f32 = jnp.float32
     shape, dma = jax.ShapeDtypeStruct, pltpu.SemaphoreType.DMA
 
@@ -574,14 +582,13 @@
             vmem(2 * bands, length_x, rows, width),
             vmem(bands, length_x, rows, width),
             vmem(2, part, length_z),
-            vmem(2, part, lanes),
+            vmem(10, part, lanes),
             vmem(tiles, 3, 2, number, tile, width),
             vmem(tiles, 2, number, tile, length_z),
             vmem(groups, 3, 4, span, lanes),
             vmem(groups, 4, span, lanes),
-            vmem(groups, places, 4, rows, lanes),
-            vmem(groups, places, 4, rows, lanes),
-            vmem(groups, 4, span, lanes),
+            vmem(groups, 2, 2, span, lanes),
+            vmem(groups, 2, 2, span, lanes),
             vmem(groups, 2, 4, span, lanes),
             vmem(groups, 2, 4, span, lanes),
             vmem(3, 2, number, part, width),
@@ -596,7 +603,7 @@
             dma((2 * bands,)),
         ]
         + [dma((tiles,))] * 2
-        + [dma((groups, places - 1))] * 4
+        + [dma((2 * groups,))] * 2
         + [dma((groups,))] * 2
         + [dma((tiles,))] * 2
         + [dma((peers,))] * 2,

time: 63 us -> 61.8 us (0.981)
  Pallas kernels: 62.8 us -> 61.7 us
    pallas_call x1, Pallas kernels: 57.5 us -> 56.3 us  [on_device(): pl.pallas_call(functools.partial(solve_all, blocks, parts), in_specs=[any...]
where the time goes in v1:
time: 61.8 us; the launch traced here: 61.7 us
  Pallas kernels  61.7 us (100%)
    pallas_call x1, Pallas kernels, on_device(): pl.pallas_call(functools.partial(solve_all, blocks, parts), in_specs=[any...  56.3 us
    pallas_call x1, Pallas kernels, on_device(): pl.pallas_call(scale, grid=(pieces,), in_specs=[inside, inside], out_spec...  5.37 us

profile of v1, /device:TPU:0, one launch (start us, length us, event | category | flops | bytes accessed | tf_op | source)
XLA Modules:
  0.0 61.7 jit_solution(3406775545161197007)
XLA Ops:
  0.0 56.3 %solve_all.1 = (f32[4,2,256,8,128]{4,3,2,1,0:T(8,128)S(1)}, f32[8,128]{1,0:T(8,128)S(1)}) custom-call(f32[2,256,32,128]{3,2,1,0:T(8,128)} %source_ref.1, f32[256,32,128]{2,1,0:T(8,128)} %speed_ref.1, f32[2,256,256]{2,1,0:T(8,128)} %constant.6.clone.roots_ref, bf16[256,256]{1,0:T(8,128)(2,1)} %constant.7.clone.x_high_ref.z_high_ref, ...), custom_call_target="tpu_custom_call" | custom-call | tf_op jit(solution)/shard_map/solve_all/pallas_call | solution.py:576
  56.3 5.4 %scale.1 = f32[2,256,32,128]{3,2,1,0:T(8,128)} custom-call(f32[8,128]{1,0:T(8,128)S(1)} %get-tuple-element.7.total_ref, f32[4,2,256,8,128]{4,3,2,1,0:T(8,128)S(1)} %get-tuple-element.8.w_ref), custom_call_target="tpu_custom_call" | custom-call | tf_op jit(solution)/shard_map/scale/pallas_call | solution.py:616

commit v2 on v1

--- a/solution.py
+++ b/solution.py
@@ -125,7 +125,7 @@
     slots,
     x_halves,
     z_halves,
-    sums_ref,
+    squares_ref,
     heard,
     source_sem,
     speed_sem,
@@ -435,6 +435,23 @@
     def _(i):
         send_in(i).wait_recv()
 
+    group = 8
+    squares_ref[...] = jnp.zeros_like(squares_ref)
+
+    def prepare(y):
+        load_speed(y).wait()
+
+        def step(i, square):
+            some = pl.ds(i * group, group)
+            v = speed[y, some]
+            speed[y, some] = wave_square - wave_square / (v * v)
+            s_re, s_im = source[y, some], source[bands + y, some]
+            return square + jnp.sum(s_re * s_re + s_im * s_im, axis=0)
+
+        squares_ref[...] += lax.fori_loop(
+            0, length // group, step, jnp.zeros((rows, lanes), jnp.float32), unroll=2
+        )
+
     lag = 2
 
     @pl.loop(0, groups)
@@ -451,6 +468,7 @@
     stages = [(2.9, merge, k) for k in range(max(groups - lag, 0), groups)]
     stages += [(5.2, relay, k) for k in range(groups)]
     stages += [(8.7, expand, k) for k in range(min(early, groups))]
+    stages += [(5.1, prepare, k) for k in range(bands)]
     for _, stage, k in sorted(stages, key=lambda item: 1.8 * item[2] + item[0]):
         stage(k)
 
@@ -485,77 +503,103 @@
     def _(i):
         send_out(i).wait_recv()
 
-    sums_ref[...] = jnp.zeros_like(sums_ref)
-    group = 8
-
-    @pl.loop(0, bands)
-    def _(y):
-        load_speed(y).wait()
+    def transform(y, j):
         flat = image.at[y].reshape(2 * length * rows, lanes)
         for c in range(2):
-            for j in range(0, rows, 2):
-                pieces = [
-                    jnp.concatenate([slots[h, c, y * rows + j + k] for h in range(parts)], axis=0)
-                    for k in range(2)
+            pieces = [
+                jnp.concatenate([slots[h, c, y * rows + j + k] for h in range(parts)], axis=0)
+                for k in range(2)
+            ]
+            result = dot_three(x_table, halves(jnp.concatenate(pieces, axis=1)))
+            for k in range(2):
+                flat[pl.ds(c * length * rows + j + k, length, stride=rows), :] = result[
+                    :, k * lanes : (k + 1) * lanes
                 ]
-                result = dot_three(x_table, halves(jnp.concatenate(pieces, axis=1)))
-                for k in range(2):
-                    flat[pl.ds(c * length * rows + j + k, length, stride=rows), :] = result[
-                        :, k * lanes : (k + 1) * lanes
-                    ]
-
-        def step(i, sums):
-            some = pl.ds(i * group, group)
-            v = speed[y, some]
-            shift = wave_square - wave_square / (v * v)
-            s_re, s_im = source[y, some], source[bands + y, some]
-            w_re, w_im = image[y, 0, some], image[y, 1, some]
-            u_re = s_re + shift * w_re + damped * w_im
-            u_im = s_im + shift * w_im - damped * w_re
-            terms = (
-                s_re * s_re + s_im * s_im,
-                s_re * u_re + s_im * u_im,
-                s_re * u_im - s_im * u_re,
-                u_re * u_re + u_im * u_im,
-            )
-            return tuple(a + jnp.sum(b, axis=0) for a, b in zip(sums, terms))
-
-        none = jnp.zeros((rows, lanes), jnp.float32)
-        sums = lax.fori_loop(0, length // group, step, (none,) * 4)
-        for k in range(4):
-            sums_ref[pl.ds(k, 1)] += jnp.sum(sums[k], axis=0, keepdims=True)
-
+
+    def tally(y, i, sums):
+        some = pl.ds(i * group, group)
+        shift = speed[y, some]
+        s_re, s_im = source[y, some], source[bands + y, some]
+        w_re, w_im = image[y, 0, some], image[y, 1, some]
+        u_re = s_re + shift * w_re + damped * w_im
+        u_im = s_im + shift * w_im - damped * w_re
+        terms = (
+            s_re * u_re + s_im * u_im,
+            s_re * u_im - s_im * u_re,
+            u_re * u_re + u_im * u_im,
+        )
+        return tuple(a + jnp.sum(b, axis=0) for a, b in zip(sums, terms))
+
+    pairs, runs = rows // 2, length // group
+
+    def both(y, sums):
+        for n in range(pairs):
+            for i in range(n * runs // pairs, (n + 1) * runs // pairs):
+                sums = tally(y - 1, i, sums)
+            transform(y, 2 * n)
+        return sums
+
+    for n in range(pairs):
+        transform(0, 2 * n)
+    sums = lax.fori_loop(1, bands, both, (jnp.zeros((rows, lanes), jnp.float32),) * 3)
+    sums = lax.fori_loop(0, runs, functools.partial(tally, bands - 1), sums, unroll=2)
+    sums = [jnp.sum(a, axis=0, keepdims=True) for a in (squares_ref[...],) + sums]
+    lane = lax.broadcasted_iota(jnp.int32, (1, lanes), 1)
+    packed = jnp.zeros((1, lanes), jnp.float32)
+    for k, row in enumerate(sums):
+        for shift in (lanes // 2, lanes // 4):
+            row = row + pltpu.roll(row, shift, 1)
+        packed = jnp.where(lax.div(lane, lanes // 4) == k, row, packed)
+    own = len(everyone)
+    heard[own : own + 1] = packed
     copies = [
-        remote(sums_ref, heard.at[k], sum_send, sum_recv, k, peer) for k, peer in enumerate(everyone)
+        remote(heard.at[own : own + 1], heard.at[k : k + 1], sum_send, sum_recv, k, peer)
+        for k, peer in enumerate(everyone)
     ]
     for copy in copies:
         copy.start()
     for copy in copies:
         copy.wait()
-    total_ref[...] = sums_ref[...] + jnp.sum(heard[...], axis=0)
+    total_ref[...] = jnp.broadcast_to(jnp.sum(heard[...], axis=0, keepdims=True), total_ref.shape)
 
     @pl.loop(0, steps)
     def _(i):
         send_out(i).wait_send()
 
 
-def scale(total_ref, w_ref, out_ref):
-    sums = jnp.sum(total_ref[...], axis=1, keepdims=True)
-    size = sums[0:1] + epsilon
-    one_re, one_im, squares = sums[1:2] / size, sums[2:3] / size, sums[3:4] / size
+def scale(total_ref, w_ref, out_ref, scaled, sems):
+    bands, _, length, _, _ = w_ref.shape
+    pieces = sems.shape[0]
+    depth = length // pieces
+    row = total_ref[0:1]
+    lane = lax.div(lax.broadcasted_iota(jnp.int32, row.shape, 1), lanes // 4)
+    sums = [jnp.sum(jnp.where(lane == k, row, 0.0), axis=1, keepdims=True) for k in range(4)]
+    size = sums[0] + epsilon
+    one_re, one_im, squares = sums[1] / size, sums[2] / size, sums[3] / size
     one = one_re * one_re + one_im * one_im
     denominator = squares - one * (epsilon / size) + epsilon
     re = jnp.broadcast_to(one_re / denominator, (rows, lanes))
     im = jnp.broadcast_to(-one_im / denominator, (rows, lanes))
-    bands, depth = w_ref.shape[0], out_ref.shape[1]
-    base = pl.program_id(0) * depth
-
-    @pl.loop(0, depth, unroll=4)
-    def _(x):
-        for y in range(bands):
-            w_re, w_im = w_ref[y, 0, base + x], w_ref[y, 1, base + x]
-            out_ref[0, x, y * rows : (y + 1) * rows] = re * w_re - im * w_im
-            out_ref[1, x, y * rows : (y + 1) * rows] = re * w_im + im * w_re
+
+    def save(i):
+        part = pl.ds(i * depth, depth)
+        return pltpu.make_async_copy(scaled.at[:, part], out_ref.at[:, part], sems.at[i])
+
+    @pl.loop(0, pieces)
+    def _(i):
+        @pl.loop(0, depth, unroll=4)
+        def _(j):
+            x = i * depth + j
+            for y in range(bands):
+                w_re, w_im = w_ref[y, 0, x], w_ref[y, 1, x]
+                scaled[0, x, y * rows : (y + 1) * rows] = re * w_re - im * w_im
+                scaled[1, x, y * rows : (y + 1) * rows] = re * w_im + im * w_re
+
+        save(i).start()
+
+    @pl.loop(0, pieces)
+    def _(i):
+        save(i).wait()
 
 
 def on_device(blocks, parts, source, speed):
@@ -595,7 +639,7 @@
             pltpu.VMEM((2, length_x, length_x), jnp.bfloat16),
             pltpu.VMEM((2, length_z, length_z), jnp.bfloat16),
             vmem(rows, width),
-            vmem(peers, rows, width),
+            vmem(peers + 1, width),
             dma((2 * bands,)),
             dma((bands,)),
             dma((5,)),
@@ -612,16 +656,14 @@
         ),
         name="solve_all",
     )(source, speed, root_table(length_x, length_z), *sine_table(length_x), *sine_table(length_z))
-    pieces = 8
+    pieces = 16
     return pl.pallas_call(
         scale,
-        grid=(pieces,),
         in_specs=[inside, inside],
-        out_specs=pl.BlockSpec((2, length_x // pieces, number, width), lambda i: (0, i, 0, 0)),
+        out_specs=anywhere,
         out_shape=shape(source.shape, f32),
-        compiler_params=pltpu.CompilerParams(
-            dimension_semantics=("arbitrary",), vmem_limit_bytes=16 * 1024 * 1024
-        ),
+        scratch_shapes=[vmem(*source.shape), dma((pieces,))],
+        compiler_params=pltpu.CompilerParams(vmem_limit_bytes=20 * 1024 * 1024),
         name="scale",
     )(sums, image)
 

time: 61.8 us -> 57.3 us (0.927)
  Pallas kernels: 61.7 us -> 57.2 us
    pallas_call x1, Pallas kernels: 56.3 us -> 53.6 us  [on_device(): pl.pallas_call(functools.partial(solve_all, blocks, parts), in_specs=[any...]
    pallas_call x1, Pallas kernels: 5.37 us -> 3.58 us  [on_device(): pl.pallas_call(scale, in_specs=[inside, inside], out_specs=anywhere, out_...]
where the time goes in v2:
time: 57.3 us; the launch traced here: 57.2 us
  Pallas kernels  57.2 us (100%)
    pallas_call x1, Pallas kernels, on_device(): pl.pallas_call(functools.partial(solve_all, blocks, parts), in_specs=[any...  53.6 us
    pallas_call x1, Pallas kernels, on_device(): pl.pallas_call(scale, in_specs=[inside, inside], out_specs=anywhere, out_...  3.58 us

profile of v2, /device:TPU:0, one launch (start us, length us, event | category | flops | bytes accessed | tf_op | source)
XLA Modules:
  0.0 57.2 jit_solution(10687640288790098438)
XLA Ops:
  0.0 53.6 %solve_all.1 = (f32[4,2,256,8,128]{4,3,2,1,0:T(8,128)S(1)}, f32[8,128]{1,0:T(8,128)S(1)}) custom-call(f32[2,256,32,128]{3,2,1,0:T(8,128)} %source_ref.1, f32[256,32,128]{2,1,0:T(8,128)} %speed_ref.1, f32[2,256,256]{2,1,0:T(8,128)} %constant.6.clone.roots_ref, bf16[256,256]{1,0:T(8,128)(2,1)} %constant.7.clone.x_high_ref.z_high_ref, ...), custom_call_target="tpu_custom_call" | custom-call | tf_op jit(solution)/shard_map/solve_all/pallas_call | solution.py:620
  53.6 3.6 %scale.1 = f32[2,256,32,128]{3,2,1,0:T(8,128)} custom-call(f32[8,128]{1,0:T(8,128)S(1)} %get-tuple-element.7.total_ref, f32[4,2,256,8,128]{4,3,2,1,0:T(8,128)S(1)} %get-tuple-element.8.w_ref), custom_call_target="tpu_custom_call" | custom-call | tf_op jit(solution)/shard_map/scale/pallas_call | solution.py:660

commit v3 on v2

--- a/solution.py
+++ b/solution.py
@@ -115,7 +115,10 @@
     roots,
     rates,
     tiles,
-    modes,
+    even_modes,
+    odd_modes,
+    even_work,
+    odd_work,
     ends,
     pair,
     waves_out,
@@ -147,7 +150,7 @@
     _, length, _, _ = source.shape
     bands = number // rows
     part = length // parts
-    length_z = modes.shape[-1]
+    length_z = even_modes.shape[-1]
     groups, _, _, span, _ = ends.shape
     per, places = span // tile, blocks // 2
     me = lax.axis_index("px")
@@ -283,28 +286,29 @@
         part = pl.ds(pl.multiple_of(i * tile, tile), tile)
         return roots[0, part], roots[1, part]
 
-    def forward(k, i):
-        s = k * per + i
+    modes, work = (even_modes, odd_modes), (even_work, odd_work)
+
+    def transform_z(p, odd):
         for c in range(2):
-            pieces = [tiles[s, h, c].reshape(number * tile, lanes) for h in range(parts)]
+            pieces = [tiles[2 * p + odd, h, c].reshape(number * tile, lanes) for h in range(parts)]
             result = dot_three(halves(jnp.concatenate(pieces, axis=1)), table)
-            modes[s, c] = result.reshape(number, tile, length_z)
+            modes[odd][p, c] = result.reshape(number, tile, length_z)
+
+    def sweep(p, odd):
+        s = 2 * p + odd
+        k, i = lax.div(s, per), lax.rem(s, per)
         root = tile_root(s)
-
-        def step(j, state):
-            first, last = state
+        first, last = (zero, zero), (zero, zero)
+        for j in range(number):
             back = number - 1 - j
-            last = plus(times(root, last), (modes[s, 0, j], modes[s, 1, j]))
-            first = plus(times(root, first), (modes[s, 0, back], modes[s, 1, back]))
-            return first, last
-
-        first, last = lax.fori_loop(0, number, step, ((zero, zero), (zero, zero)), unroll=4)
+            last = plus(times(root, last), (modes[odd][p, 0, j], modes[odd][p, 1, j]))
+            first = plus(times(root, first), (modes[odd][p, 0, back], modes[odd][p, 1, back]))
         part = pl.ds(pl.multiple_of(i * tile, tile), tile)
         for h in range(2):
             slot = slot_of(h, side)
             for plane, value in enumerate(first + last):
                 ends[k, slot, plane, part] = value[:, h * lanes : (h + 1) * lanes]
-        send_ends(k, i).start()
+        return send_ends(k, i)
 
     def either(a, b):
         return tuple(jnp.where(behind == 0, x, y) for x, y in zip(a, b))
@@ -367,69 +371,36 @@
         spot = pl.ds(pl.multiple_of(i * tile, tile), tile)
         return remote(slots.at[2, :, :, spot], slots.at[mine, :, :, spot], out_send, out_recv, i, beside)
 
-    wide = 2 if per % 2 == 0 else 1
-
-    def backward(k, i):
-        spots = [i * wide + n for n in range(wide)]
-        tiles_here = [k * per + spot for spot in spots]
-        own = [tile_root(s) for s in tiles_here]
-
-        def side_of(plane):
-            return [
-                tuple(
-                    jnp.concatenate(
-                        [
-                            edges[k, h, plane + c, pl.ds(pl.multiple_of(spot * tile, tile), tile)]
-                            for h in range(2)
-                        ],
-                        axis=1,
-                    )
-                    for c in range(2)
-                )
-                for spot in spots
-            ]
-
-        before, after = side_of(0), side_of(2)
-
-        def mode(s, j):
-            return modes[s, 0, j], modes[s, 1, j]
-
-        def keep(s, j, value):
-            modes[s, 0, j] = value[0]
-            modes[s, 1, j] = value[1]
-
-        def ahead(j, states):
-            states = [plus(times(r, v), mode(s, j)) for s, r, v in zip(tiles_here, own, states)]
-            for s, value in zip(tiles_here, states):
-                keep(s, j, value)
-            return states
-
-        lasts = lax.fori_loop(0, number, ahead, before, unroll=2)
-        values = []
-        for root, last, far in zip(own, lasts, after):
-            square = times(root, root)
-            scaled = times(root, inverse((1.0 - square[0], -square[1])))
-            values.append(times(scaled, plus(times(root, last), far)))
-
-        def back(j, values):
-            j = number - 1 - j
-            values = [times(r, plus(v, mode(s, j))) for s, r, v in zip(tiles_here, own, values)]
-            for s, value in zip(tiles_here, values):
-                keep(s, j, value)
-            return values
-
-        lax.fori_loop(0, number, back, values, unroll=2)
-
-        @pl.loop(0, wide)
-        def _(n):
-            s = k * per + i * wide + n
-            for c in range(2):
-                result = dot_three(halves(modes[s, c].reshape(number * tile, length_z)), table)
-                spot = pl.ds(pl.multiple_of(s * tile, tile), tile)
-                for h in range(parts):
-                    block = result[:, h * lanes : (h + 1) * lanes]
-                    slots[slot_of(h, mine), c, :, spot] = block.reshape(number, tile, lanes)
-            send_out(s).start()
+    def solve_y(p, odd):
+        s = 2 * p + odd
+        k, i = lax.div(s, per), lax.rem(s, per)
+        root = tile_root(s)
+        part = pl.ds(pl.multiple_of(i * tile, tile), tile)
+        carried = [
+            jnp.concatenate([edges[k, h, plane, part] for h in range(2)], axis=1) for plane in range(4)
+        ]
+        state, after = tuple(carried[:2]), tuple(carried[2:])
+        for j in range(number):
+            state = plus(times(root, state), (modes[odd][p, 0, j], modes[odd][p, 1, j]))
+            work[odd][0, j] = state[0]
+            work[odd][1, j] = state[1]
+        square = times(root, root)
+        scaled = times(root, inverse((1.0 - square[0], -square[1])))
+        value = times(scaled, plus(times(root, state), after))
+        for j in range(number - 1, -1, -1):
+            value = times(root, plus(value, (work[odd][0, j], work[odd][1, j])))
+            work[odd][0, j] = value[0]
+            work[odd][1, j] = value[1]
+
+    def emit(p, odd):
+        s = 2 * p + odd
+        spot = pl.ds(pl.multiple_of(s * tile, tile), tile)
+        for c in range(2):
+            result = dot_three(halves(work[odd][c].reshape(number * tile, length_z)), table)
+            for h in range(parts):
+                block = result[:, h * lanes : (h + 1) * lanes]
+                slots[slot_of(h, mine), c, :, spot] = block.reshape(number, tile, lanes)
+        return send_out(s)
 
     @pl.loop(0, 2 * bands)
     def _(i):
@@ -454,16 +425,32 @@
 
     lag = 2
 
-    @pl.loop(0, groups)
-    def _(k):
-        @pl.loop(0, per)
-        def _(i):
-            forward(k, i)
-
-        @pl.when(k >= lag)
+    duos = steps // 2
+    duos_of = per // 2
+
+    def ready(p):
+        @pl.when(jnp.logical_and(lax.rem(p + 1, duos_of) == 0, lax.div(p, duos_of) >= lag))
         def _():
-            merge(k - lag)
-
+            merge(lax.div(p, duos_of) - lag)
+
+    transform_z(0, 0)
+
+    @pl.loop(0, duos - 1)
+    def _(p):
+        copy = sweep(p, 0)
+        transform_z(p, 1)
+        copy.start()
+        copy = sweep(p, 1)
+        transform_z(p + 1, 0)
+        copy.start()
+        ready(p)
+
+    copy = sweep(duos - 1, 0)
+    transform_z(duos - 1, 1)
+    copy.start()
+    sweep(duos - 1, 1).start()
+    if groups > lag:
+        merge(groups - 1 - lag)
     early = 3
     stages = [(2.9, merge, k) for k in range(max(groups - lag, 0), groups)]
     stages += [(5.2, relay, k) for k in range(groups)]
@@ -472,32 +459,31 @@
     for _, stage, k in sorted(stages, key=lambda item: 1.8 * item[2] + item[0]):
         stage(k)
 
-    @pl.loop(0, groups)
-    def _(k):
-        send_edges(k).wait_recv()
-
-        @pl.loop(0, per // wide)
-        def _(i):
-            backward(k, i)
-
-        @pl.when(k + early < groups)
+    send_edges(0).wait_recv()
+    solve_y(0, 0)
+    solve_y(0, 1)
+    emit(0, 0).start()
+
+    @pl.loop(1, duos)
+    def _(p):
+        k = lax.div(p, duos_of)
+
+        @pl.when(lax.rem(p, duos_of) == 0)
         def _():
-            expand(k + early)
-
-    @pl.loop(0, groups)
-    def _(k):
-        send_edges(k).wait_send()
-        send_inward(k).wait_send()
-        for i in range(per):
-            send_ends(k, i).wait_send()
-
-        @pl.when(depth > 0)
-        def _():
-            send_outward(k).wait_send()
-
-    @pl.loop(0, 2 * bands)
-    def _(i):
-        send_in(i).wait_send()
+            @pl.when(k - 1 + early < groups)
+            def _():
+                expand(k - 1 + early)
+
+            send_edges(k).wait_recv()
+
+        copy = emit(p - 1, 1)
+        solve_y(p, 0)
+        copy.start()
+        copy = emit(p, 0)
+        solve_y(p, 1)
+        copy.start()
+
+    emit(duos - 1, 1).start()
 
     @pl.loop(0, steps)
     def _(i):
@@ -558,13 +544,29 @@
     ]
     for copy in copies:
         copy.start()
+
+    @pl.loop(0, groups)
+    def _(k):
+        send_edges(k).wait_send()
+        send_inward(k).wait_send()
+        for i in range(per):
+            send_ends(k, i).wait_send()
+
+        @pl.when(depth > 0)
+        def _():
+            send_outward(k).wait_send()
+
+    @pl.loop(0, 2 * bands)
+    def _(i):
+        send_in(i).wait_send()
+
+    @pl.loop(0, steps)
+    def _(i):
+        send_out(i).wait_send()
+
     for copy in copies:
         copy.wait()
     total_ref[...] = jnp.broadcast_to(jnp.sum(heard[...], axis=0, keepdims=True), total_ref.shape)
-
-    @pl.loop(0, steps)
-    def _(i):
-        send_out(i).wait_send()
 
 
 def scale(total_ref, w_ref, out_ref, scaled, sems):
@@ -628,7 +630,10 @@
             vmem(2, part, length_z),
             vmem(10, part, lanes),
             vmem(tiles, 3, 2, number, tile, width),
-            vmem(tiles, 2, number, tile, length_z),
+            vmem(tiles // 2, 2, number, tile, length_z),
+            vmem(tiles // 2, 2, number, tile, length_z),
+            vmem(2, number, tile, length_z),
+            vmem(2, number, tile, length_z),
             vmem(groups, 3, 4, span, lanes),
             vmem(groups, 4, span, lanes),
             vmem(groups, 2, 2, span, lanes),

time: 57.3 us -> 54.9 us (0.958)
  Pallas kernels: 57.2 us -> 54.8 us
    pallas_call x1, Pallas kernels: 53.6 us -> 51.2 us  [on_device(): pl.pallas_call(functools.partial(solve_all, blocks, parts), in_specs=[any...]
where the time goes in v3:
time: 54.9 us; the launch traced here: 54.8 us
  Pallas kernels  54.8 us (100%)
    pallas_call x1, Pallas kernels, on_device(): pl.pallas_call(functools.partial(solve_all, blocks, parts), in_specs=[any...  51.2 us
    pallas_call x1, Pallas kernels, on_device(): pl.pallas_call(scale, in_specs=[inside, inside], out_specs=anywhere, out_...  3.58 us

profile of v3, /device:TPU:0, one launch (start us, length us, event | category | flops | bytes accessed | tf_op | source)
XLA Modules:
  0.0 54.8 jit_solution(10489864079583182662)
XLA Ops:
  0.0 51.2 %solve_all.1 = (f32[4,2,256,8,128]{4,3,2,1,0:T(8,128)S(1)}, f32[8,128]{1,0:T(8,128)S(1)}) custom-call(f32[2,256,32,128]{3,2,1,0:T(8,128)} %source_ref.1, f32[256,32,128]{2,1,0:T(8,128)} %speed_ref.1, f32[2,256,256]{2,1,0:T(8,128)} %constant.6.clone.roots_ref, bf16[256,256]{1,0:T(8,128)(2,1)} %constant.7.clone.x_high_ref.z_high_ref, ...), custom_call_target="tpu_custom_call" | custom-call | tf_op jit(solution)/shard_map/solve_all/pallas_call | solution.py:622
  51.2 3.6 %scale.1 = f32[2,256,32,128]{3,2,1,0:T(8,128)} custom-call(f32[8,128]{1,0:T(8,128)S(1)} %get-tuple-element.7.total_ref, f32[4,2,256,8,128]{4,3,2,1,0:T(8,128)S(1)} %get-tuple-element.8.w_ref), custom_call_target="tpu_custom_call" | custom-call | tf_op jit(solution)/shard_map/scale/pallas_call | solution.py:665

commit v4 on v3

--- a/solution.py
+++ b/solution.py
@@ -123,6 +123,9 @@
     pair,
     waves_out,
     waves,
+    tops,
+    outs,
+    met,
     inner,
     edges,
     slots,
@@ -139,6 +142,10 @@
     ends_recv,
     wave_send,
     wave_recv,
+    top_send,
+    top_recv,
+    outs_send,
+    outs_recv,
     edge_send,
     edge_recv,
     out_send,
@@ -162,6 +169,7 @@
     behind = lax.div(place, depths)
     depth = place + behind * (places - 1 - 2 * place)
     inmost = lax.div(depth + 1, depths)
+    others = [lax.rem(place + k, places) for k in range(1, places)]
     toward = 1 - 2 * behind
     everyone = []
     for k in range(1, blocks * parts):
@@ -259,24 +267,41 @@
             {"px": other},
         )
 
-    def wave(k, way, slot, place):
+    def wave(k, place):
+        return remote(
+            waves_out.at[k, 0], waves.at[k], wave_send, wave_recv, k, {"px": 2 * place + side}
+        )
+
+    def send_top(k, i, from_side):
         return pltpu.make_async_remote_copy(
-            src_ref=waves_out.at[k, way],
-            dst_ref=waves.at[k, slot],
-            send_sem=wave_send.at[2 * k + way],
-            recv_sem=wave_recv.at[2 * k + slot],
-            device_id={"px": 2 * place + side},
+            src_ref=tops.at[k, from_side],
+            dst_ref=tops.at[k, from_side],
+            send_sem=top_send.at[k, i],
+            recv_sem=top_recv.at[k, from_side],
+            device_id={"px": 2 * others[i] + side},
             device_id_type=MESH,
         )
 
-    def send_inward(k):
-        return wave(k, 0, inmost, place + toward)
-
-    def send_outward(k):
-        return wave(k, 1, 1, place - toward)
-
-    def send_edges(k):
-        return remote(inner.at[k, 1 - side], edges.at[k, side], edge_send, edge_recv, k, {"px": other})
+    def send_outs(k, to_depth, from_depth):
+        return pltpu.make_async_remote_copy(
+            src_ref=waves_out.at[k, 1],
+            dst_ref=outs.at[k, from_depth],
+            send_sem=outs_send.at[k, to_depth],
+            recv_sem=outs_recv.at[k, from_depth],
+            device_id={"px": 2 * (to_depth + behind * (places - 1 - 2 * to_depth)) + side},
+            device_id_type=MESH,
+        )
+
+    def send_edges(k, i):
+        spot = pl.ds(pl.multiple_of(i * tile, tile), tile)
+        return remote(
+            inner.at[k, 1 - side, :, spot],
+            edges.at[k, side, :, spot],
+            edge_send,
+            edge_recv,
+            k * per + i,
+            {"px": other},
+        )
 
     def group_rates(k, *which):
         part = pl.ds(k * span, span) if isinstance(k, int) else pl.ds(pl.multiple_of(k * span, span), span)
@@ -316,9 +341,19 @@
     def pass_inward(k, rate, echo, came):
         bounced = times(echo, pair_of(pair.at[k], 2))
         value = plus(pair_of(pair.at[k]), times(rate, plus(came, bounced)))
-        for c in range(2):
-            waves_out[k, 0, c] = value[c]
-        send_inward(k).start()
+
+        @pl.when(inmost == 0)
+        def _():
+            for c in range(2):
+                waves_out[k, 0, c] = value[c]
+            wave(k, place + toward).start()
+
+        @pl.when(inmost == 1)
+        def _():
+            for c in range(2):
+                tops[k, behind, c] = value[c]
+            for i in range(places - 1):
+                send_top(k, i, behind).start()
 
     def merge(k):
         for i in range(per):
@@ -329,42 +364,62 @@
         for plane, value in enumerate(either(last, first) + either(first, last)):
             pair[k, plane] = value
 
+        @pl.when(depth > 0)
+        def _():
+            for c in range(2):
+                waves_out[k, 1, c] = pair[k, 2 + c]
+
+        for n in range(depths - 1):
+
+            @pl.when(depth > n)
+            def _():
+                send_outs(k, n, depth).start()
+
         @pl.when(depth == 0)
         def _():
             none = jnp.zeros((span, lanes), jnp.float32)
             for c in range(2):
-                waves[k, 0, c] = none
+                waves[k, c] = none
             pass_inward(k, rate, echo, (none, none))
 
     def relay(k):
         @pl.when(depth > 0)
         def _():
-            wave(k, 0, 0, place - toward).wait_recv()
+            wave(k, place - toward).wait_recv()
             rate, echo = group_rates(k, 1, 2)
-            pass_inward(k, rate, echo, pair_of(waves.at[k, 0]))
+            pass_inward(k, rate, echo, pair_of(waves.at[k]))
 
     def expand(k):
-        wave(k, 1, 1, place + toward).wait_recv()
+        @pl.when(inmost == 0)
+        def _():
+            send_top(k, 0, behind).wait_recv()
+
+        send_top(k, 0, 1 - behind).wait_recv()
         jump, rate, echo, whole, spread = group_rates(k, 0, 1, 2, 3, 4)
-        came = pair_of(waves.at[k, 1])
-        met = times(spread, minus(came, times(whole, pair_of(waves_out.at[k, 0]))))
-        came = tuple(jnp.where(inmost == 1, a, b) for a, b in zip(met, came))
+        ours, theirs = pair_of(tops.at[k, behind]), pair_of(tops.at[k, 1 - behind])
+        value = times(spread, minus(theirs, times(whole, ours)))
+        for c in range(2):
+            met[k, c] = value[c]
+        for n in range(depths - 1, 0, -1):
+
+            @pl.when(depth < n)
+            def _():
+                send_outs(k, 0, n).wait_recv()
+                value = plus(pair_of(outs.at[k, n]), times(rate, pair_of(met.at[k])))
+                for c in range(2):
+                    met[k, c] = value[c]
+
+        came = pair_of(met.at[k])
         out = plus(pair_of(pair.at[k], 2), times(rate, came))
-        back = plus(pair_of(waves.at[k, 0]), times(echo, out))
-
-        @pl.when(depth > 0)
-        def _():
-            for c in range(2):
-                waves_out[k, 1, c] = out[c]
-            send_outward(k).start()
-
+        back = plus(pair_of(waves.at[k]), times(echo, out))
         before, after = either(back, came), either(came, back)
         left = before + plus(pair_of(ends.at[k, 1]), times(jump, after))
         right = plus(pair_of(ends.at[k, 0], 2), times(jump, before)) + after
         for q, values in enumerate((left, right)):
             for plane, value in enumerate(values):
                 inner[k, q, plane] = value
-        send_edges(k).start()
+        for i in range(per):
+            send_edges(k, i).start()
         edges[k, side] = inner[k, side]
 
     def send_out(i):
@@ -452,17 +507,23 @@
     if groups > lag:
         merge(groups - 1 - lag)
     early = 3
-    stages = [(2.9, merge, k) for k in range(max(groups - lag, 0), groups)]
-    stages += [(5.2, relay, k) for k in range(groups)]
-    stages += [(8.7, expand, k) for k in range(min(early, groups))]
-    stages += [(5.1, prepare, k) for k in range(bands)]
-    for _, stage, k in sorted(stages, key=lambda item: 1.8 * item[2] + item[0]):
+    stages = [(2.7, merge, k) for k in range(max(groups - lag, 0), groups)]
+    stages += [(5.7, relay, k) for k in range(groups)]
+    stages += [(10.4, expand, k) for k in range(min(early, groups))]
+    stages += [(4.2, prepare, k) for k in range(bands)]
+    for _, stage, k in sorted(stages, key=lambda item: 1.55 * item[2] + item[0]):
         stage(k)
 
-    send_edges(0).wait_recv()
+    def await_edges(p, odd):
+        s = 2 * p + odd
+        send_edges(lax.div(s, per), lax.rem(s, per)).wait_recv()
+
+    await_edges(0, 0)
     solve_y(0, 0)
+    await_edges(0, 1)
+    copy = emit(0, 0)
     solve_y(0, 1)
-    emit(0, 0).start()
+    copy.start()
 
     @pl.loop(1, duos)
     def _(p):
@@ -474,11 +535,11 @@
             def _():
                 expand(k - 1 + early)
 
-            send_edges(k).wait_recv()
-
+        await_edges(p, 0)
         copy = emit(p - 1, 1)
         solve_y(p, 0)
         copy.start()
+        await_edges(p, 1)
         copy = emit(p, 0)
         solve_y(p, 1)
         copy.start()
@@ -547,14 +608,24 @@
 
     @pl.loop(0, groups)
     def _(k):
-        send_edges(k).wait_send()
-        send_inward(k).wait_send()
         for i in range(per):
             send_ends(k, i).wait_send()
-
-        @pl.when(depth > 0)
-        def _():
-            send_outward(k).wait_send()
+            send_edges(k, i).wait_send()
+
+        @pl.when(inmost == 0)
+        def _():
+            wave(k, place + toward).wait_send()
+
+        @pl.when(inmost == 1)
+        def _():
+            for i in range(places - 1):
+                send_top(k, i, behind).wait_send()
+
+        for n in range(depths - 1):
+
+            @pl.when(depth > n)
+            def _():
+                send_outs(k, n, depth).wait_send()
 
     @pl.loop(0, 2 * bands)
     def _(i):
@@ -611,7 +682,7 @@
     tile = 2 * rows
     bands, tiles = number // rows, part // tile
     span = rows * blocks // 2
-    groups, peers = part // span, blocks * parts - 1
+    groups, places, peers = part // span, blocks // 2, blocks * parts - 1
     f32 = jnp.float32
     shape, dma = jax.ShapeDtypeStruct, pltpu.SemaphoreType.DMA
 
@@ -637,7 +708,10 @@
             vmem(groups, 3, 4, span, lanes),
             vmem(groups, 4, span, lanes),
             vmem(groups, 2, 2, span, lanes),
+            vmem(groups, 2, span, lanes),
             vmem(groups, 2, 2, span, lanes),
+            vmem(groups, places // 2, 2, span, lanes),
+            vmem(groups, 2, span, lanes),
             vmem(groups, 2, 4, span, lanes),
             vmem(groups, 2, 4, span, lanes),
             vmem(3, 2, number, part, width),
@@ -652,8 +726,10 @@
             dma((2 * bands,)),
         ]
         + [dma((tiles,))] * 2
-        + [dma((2 * groups,))] * 2
         + [dma((groups,))] * 2
+        + [dma((groups, places - 1)), dma((groups, 2))]
+        + [dma((groups, places // 2))] * 2
+        + [dma((tiles,))] * 2
         + [dma((tiles,))] * 2
         + [dma((peers,))] * 2,
         compiler_params=pltpu.CompilerParams(

time: 54.9 us -> 52.8 us (0.962)
  Pallas kernels: 54.8 us -> 52.6 us
    pallas_call x1, Pallas kernels: 51.2 us -> 49 us  [on_device(): pl.pallas_call(functools.partial(solve_all, blocks, parts), in_specs=[any...]
where the time goes in v4:
time: 52.8 us; the launch traced here: 52.6 us
  Pallas kernels  52.6 us (100%)
    pallas_call x1, Pallas kernels, on_device(): pl.pallas_call(functools.partial(solve_all, blocks, parts), in_specs=[any...  49 us
    pallas_call x1, Pallas kernels, on_device(): pl.pallas_call(scale, in_specs=[inside, inside], out_specs=anywhere, out_...  3.58 us

profile of v4, /device:TPU:0, one launch (start us, length us, event | category | flops | bytes accessed | tf_op | source)
XLA Modules:
  0.0 52.6 jit_solution(1056606391782610643)
XLA Ops:
  0.0 49.0 %solve_all.1 = (f32[4,2,256,8,128]{4,3,2,1,0:T(8,128)S(1)}, f32[8,128]{1,0:T(8,128)S(1)}) custom-call(f32[2,256,32,128]{3,2,1,0:T(8,128)} %source_ref.1, f32[256,32,128]{2,1,0:T(8,128)} %speed_ref.1, f32[2,256,256]{2,1,0:T(8,128)} %constant.6.clone.roots_ref, bf16[256,256]{1,0:T(8,128)(2,1)} %constant.7.clone.x_high_ref.z_high_ref, ...), custom_call_target="tpu_custom_call" | custom-call | tf_op jit(solution)/shard_map/solve_all/pallas_call | solution.py:693
  49.1 3.6 %scale.1 = f32[2,256,32,128]{3,2,1,0:T(8,128)} custom-call(f32[8,128]{1,0:T(8,128)S(1)} %get-tuple-element.7.total_ref, f32[4,2,256,8,128]{4,3,2,1,0:T(8,128)S(1)} %get-tuple-element.8.w_ref), custom_call_target="tpu_custom_call" | custom-call | tf_op jit(solution)/shard_map/scale/pallas_call | solution.py:741

commit v5 on v4

--- a/solution.py
+++ b/solution.py
@@ -84,18 +84,25 @@
     barrier = pltpu.get_barrier_semaphore()
     for peer in peers:
         pl.semaphore_signal(barrier, inc=1, device_id=peer, device_id_type=MESH)
-    pl.semaphore_wait(barrier, len(peers))
-
-
-def remote(source, target, sends, receives, place, device):
+
+
+def await_greetings(peers):
+    pl.semaphore_wait(pltpu.get_barrier_semaphore(), len(peers))
+
+
+def between(source, target, sent, received, device):
     return pltpu.make_async_remote_copy(
         src_ref=source,
         dst_ref=target,
-        send_sem=sends.at[place],
-        recv_sem=receives.at[place],
+        send_sem=sent,
+        recv_sem=received,
         device_id=device,
         device_id_type=MESH,
     )
+
+
+def remote(source, target, sends, receives, place, device):
+    return between(source, target, sends.at[place], receives.at[place], device)
 
 
 def solve_all(
@@ -219,7 +226,7 @@
     def send_in(i):
         c, y = lax.div(i, bands), lax.rem(i, bands)
         return remote(
-            tiles.at[:, 2, c, band(y)], tiles.at[:, mine, c, band(y)], in_send, in_recv, i, beside
+            tiles.at[:, 2, c, band(y)], tiles.at[:, mine, c, band(y)], in_send, in_recv, 0, beside
         )
 
     @pl.loop(0, 2 * bands)
@@ -234,6 +241,11 @@
                 for h in range(parts):
                     block = result[h * part : (h + 1) * part, k * lanes : (k + 1) * lanes]
                     tiles[:, slot_of(h, mine), c, y * rows + j + k] = block.reshape(steps, tile, lanes)
+
+        @pl.when(i == 0)
+        def _():
+            await_greetings(everyone)
+
         send_in(i).start()
 
     for copy in tables[2:]:
@@ -258,25 +270,24 @@
 
     def send_ends(k, i):
         spot = pl.ds(pl.multiple_of(i * tile, tile), tile)
-        return remote(
+        return between(
             ends.at[k, 2, :, spot],
             ends.at[k, side, :, spot],
-            ends_send,
-            ends_recv,
-            k * per + i,
+            ends_send.at[0],
+            ends_recv.at[k],
             {"px": other},
         )
 
     def wave(k, place):
-        return remote(
-            waves_out.at[k, 0], waves.at[k], wave_send, wave_recv, k, {"px": 2 * place + side}
+        return between(
+            waves_out.at[k, 0], waves.at[k], wave_send.at[0], wave_recv.at[k], {"px": 2 * place + side}
         )
 
     def send_top(k, i, from_side):
         return pltpu.make_async_remote_copy(
             src_ref=tops.at[k, from_side],
             dst_ref=tops.at[k, from_side],
-            send_sem=top_send.at[k, i],
+            send_sem=top_send.at[i],
             recv_sem=top_recv.at[k, from_side],
             device_id={"px": 2 * others[i] + side},
             device_id_type=MESH,
@@ -286,20 +297,19 @@
         return pltpu.make_async_remote_copy(
             src_ref=waves_out.at[k, 1],
             dst_ref=outs.at[k, from_depth],
-            send_sem=outs_send.at[k, to_depth],
-            recv_sem=outs_recv.at[k, from_depth],
+            send_sem=outs_send.at[to_depth],
+            recv_sem=outs_recv.at[k, from_depth - 1],
             device_id={"px": 2 * (to_depth + behind * (places - 1 - 2 * to_depth)) + side},
             device_id_type=MESH,
         )
 
     def send_edges(k, i):
         spot = pl.ds(pl.multiple_of(i * tile, tile), tile)
-        return remote(
+        return between(
             inner.at[k, 1 - side, :, spot],
             edges.at[k, side, :, spot],
-            edge_send,
-            edge_recv,
-            k * per + i,
+            edge_send.at[0],
+            edge_recv.at[k * per + i],
             {"px": other},
         )
 
@@ -356,8 +366,9 @@
                 send_top(k, i, behind).start()
 
     def merge(k):
-        for i in range(per):
-            send_ends(k, i).wait_recv()
+        between(
+            ends.at[k, 2], ends.at[k, 1 - side], ends_send.at[0], ends_recv.at[k], {"px": other}
+        ).wait_recv()
         jump, rate, echo = group_rates(k, 0, 1, 2)
         first = plus(pair_of(ends.at[k, 0]), times(jump, pair_of(ends.at[k, 1])))
         last = plus(pair_of(ends.at[k, 1], 2), times(jump, pair_of(ends.at[k, 0], 2)))
@@ -422,9 +433,9 @@
             send_edges(k, i).start()
         edges[k, side] = inner[k, side]
 
-    def send_out(i):
+    def send_out(i, c):
         spot = pl.ds(pl.multiple_of(i * tile, tile), tile)
-        return remote(slots.at[2, :, :, spot], slots.at[mine, :, :, spot], out_send, out_recv, i, beside)
+        return remote(slots.at[2, c, :, spot], slots.at[mine, c, :, spot], out_send, out_recv, 0, beside)
 
     def solve_y(p, odd):
         s = 2 * p + odd
@@ -447,19 +458,18 @@
             work[odd][0, j] = value[0]
             work[odd][1, j] = value[1]
 
-    def emit(p, odd):
+    def emit(p, odd, parts_of=range(2)):
         s = 2 * p + odd
         spot = pl.ds(pl.multiple_of(s * tile, tile), tile)
-        for c in range(2):
+        for c in parts_of:
             result = dot_three(halves(work[odd][c].reshape(number * tile, length_z)), table)
             for h in range(parts):
                 block = result[:, h * lanes : (h + 1) * lanes]
                 slots[slot_of(h, mine), c, :, spot] = block.reshape(number, tile, lanes)
-        return send_out(s)
-
-    @pl.loop(0, 2 * bands)
-    def _(i):
-        send_in(i).wait_recv()
+        return [send_out(s, c) for c in parts_of]
+
+    all_in = remote(tiles.at[:, 2], tiles.at[:, mine], in_send, in_recv, 0, beside)
+    all_in.wait_recv()
 
     group = 8
     squares_ref[...] = jnp.zeros_like(squares_ref)
@@ -521,9 +531,10 @@
     await_edges(0, 0)
     solve_y(0, 0)
     await_edges(0, 1)
-    copy = emit(0, 0)
+    copies = emit(0, 0)
     solve_y(0, 1)
-    copy.start()
+    for copy in copies:
+        copy.start()
 
     @pl.loop(1, duos)
     def _(p):
@@ -536,19 +547,22 @@
                 expand(k - 1 + early)
 
         await_edges(p, 0)
-        copy = emit(p - 1, 1)
+        copies = emit(p - 1, 1)
         solve_y(p, 0)
-        copy.start()
+        for copy in copies:
+            copy.start()
+
         await_edges(p, 1)
-        copy = emit(p, 0)
+        copies = emit(p, 0)
         solve_y(p, 1)
-        copy.start()
-
-    emit(duos - 1, 1).start()
-
-    @pl.loop(0, steps)
-    def _(i):
-        send_out(i).wait_recv()
+        for copy in copies:
+            copy.start()
+
+    for c in range(2):
+        emit(duos - 1, 1, [c])[0].start()
+
+    all_out = remote(slots.at[2], slots.at[mine], out_send, out_recv, 0, beside)
+    all_out.wait_recv()
 
     def transform(y, j):
         flat = image.at[y].reshape(2 * length * rows, lanes)
@@ -598,46 +612,39 @@
             row = row + pltpu.roll(row, shift, 1)
         packed = jnp.where(lax.div(lane, lanes // 4) == k, row, packed)
     own = len(everyone)
-    heard[own : own + 1] = packed
+    heard[own] = packed
     copies = [
-        remote(heard.at[own : own + 1], heard.at[k : k + 1], sum_send, sum_recv, k, peer)
+        remote(heard.at[own], heard.at[k], sum_send, sum_recv, 0, peer)
         for k, peer in enumerate(everyone)
     ]
     for copy in copies:
         copy.start()
 
-    @pl.loop(0, groups)
-    def _(k):
-        for i in range(per):
-            send_ends(k, i).wait_send()
-            send_edges(k, i).wait_send()
-
-        @pl.when(inmost == 0)
-        def _():
-            wave(k, place + toward).wait_send()
-
-        @pl.when(inmost == 1)
-        def _():
-            for i in range(places - 1):
-                send_top(k, i, behind).wait_send()
-
-        for n in range(depths - 1):
-
-            @pl.when(depth > n)
-            def _():
-                send_outs(k, n, depth).wait_send()
-
-    @pl.loop(0, 2 * bands)
-    def _(i):
-        send_in(i).wait_send()
-
-    @pl.loop(0, steps)
-    def _(i):
-        send_out(i).wait_send()
-
-    for copy in copies:
-        copy.wait()
-    total_ref[...] = jnp.broadcast_to(jnp.sum(heard[...], axis=0, keepdims=True), total_ref.shape)
+    between(ends.at[:, 2], ends.at[:, side], ends_send.at[0], ends_recv.at[0], {"px": other}).wait_send()
+    between(inner.at[:, 1 - side], edges.at[:, side], edge_send.at[0], edge_recv.at[0], {"px": other}).wait_send()
+
+    @pl.when(inmost == 0)
+    def _():
+        between(waves_out.at[:, 0], waves, wave_send.at[0], wave_recv.at[0], {"px": other}).wait_send()
+
+    @pl.when(inmost == 1)
+    def _():
+        for i in range(places - 1):
+            ours = tops.at[:, behind]
+            between(ours, ours, top_send.at[i], top_recv.at[0, 0], {"px": other}).wait_send()
+
+    for n in range(depths - 1):
+
+        @pl.when(depth > n)
+        def _():
+            sent = waves_out.at[:, 1]
+            between(sent, outs.at[:, 0], outs_send.at[n], outs_recv.at[0, 0], {"px": other}).wait_send()
+
+    all_in.wait_send()
+    all_out.wait_send()
+    rest = heard.at[0:own]
+    remote(rest, rest, sum_send, sum_recv, 0, everyone[0]).wait()
+    total_ref[...] = jnp.broadcast_to(jnp.sum(heard[...], axis=0), total_ref.shape)
 
 
 def scale(total_ref, w_ref, out_ref, scaled, sems):
@@ -718,20 +725,27 @@
             pltpu.VMEM((2, length_x, length_x), jnp.bfloat16),
             pltpu.VMEM((2, length_z, length_z), jnp.bfloat16),
             vmem(rows, width),
-            vmem(peers + 1, width),
+            vmem(peers + 1, 1, width),
             dma((2 * bands,)),
             dma((bands,)),
             dma((5,)),
-            dma((2 * bands,)),
-            dma((2 * bands,)),
-        ]
-        + [dma((tiles,))] * 2
-        + [dma((groups,))] * 2
-        + [dma((groups, places - 1)), dma((groups, 2))]
-        + [dma((groups, places // 2))] * 2
-        + [dma((tiles,))] * 2
-        + [dma((tiles,))] * 2
-        + [dma((peers,))] * 2,
+            dma((1,)),
+            dma((1,)),
+            dma((1,)),
+            dma((groups,)),
+            dma((1,)),
+            dma((groups,)),
+            dma((places - 1,)),
+            dma((groups, 2)),
+            dma((places // 2,)),
+            dma((groups, places // 2 - 1)),
+            dma((1,)),
+            dma((tiles,)),
+            dma((1,)),
+            dma((1,)),
+            dma((1,)),
+            dma((1,)),
+        ],
         compiler_params=pltpu.CompilerParams(
             vmem_limit_bytes=55 * 1024 * 1024, collective_id=0, has_side_effects=True
         ),

time: 52.8 us -> 52.1 us (0.987)
  Pallas kernels: 52.6 us -> 51.9 us
    pallas_call x1, Pallas kernels: 49 us -> 48.4 us  [on_device(): pl.pallas_call(functools.partial(solve_all, blocks, parts), in_specs=[any...]
where the time goes in v5:
time: 52.1 us; the launch traced here: 51.9 us
  Pallas kernels  51.9 us (100%)
    pallas_call x1, Pallas kernels, on_device(): pl.pallas_call(functools.partial(solve_all, blocks, parts), in_specs=[any...  48.4 us
    pallas_call x1, Pallas kernels, on_device(): pl.pallas_call(scale, in_specs=[inside, inside], out_specs=anywhere, out_...  3.58 us

profile of v5, /device:TPU:0, one launch (start us, length us, event | category | flops | bytes accessed | tf_op | source)
XLA Modules:
  0.0 51.9 jit_solution(7788475351761371214)
XLA Ops:
  0.0 48.4 %solve_all.1 = (f32[4,2,256,8,128]{4,3,2,1,0:T(8,128)S(1)}, f32[8,128]{1,0:T(8,128)S(1)}) custom-call(f32[2,256,32,128]{3,2,1,0:T(8,128)} %source_ref.1, f32[256,32,128]{2,1,0:T(8,128)} %speed_ref.1, f32[2,256,256]{2,1,0:T(8,128)} %constant.6.clone.roots_ref, bf16[256,256]{1,0:T(8,128)(2,1)} %constant.7.clone.x_high_ref.z_high_ref, ...), custom_call_target="tpu_custom_call" | custom-call | tf_op jit(solution)/shard_map/solve_all/pallas_call | solution.py:700
  48.4 3.6 %scale.1 = f32[2,256,32,128]{3,2,1,0:T(8,128)} custom-call(f32[8,128]{1,0:T(8,128)S(1)} %get-tuple-element.7.total_ref, f32[4,2,256,8,128]{4,3,2,1,0:T(8,128)S(1)} %get-tuple-element.8.w_ref), custom_call_target="tpu_custom_call" | custom-call | tf_op jit(solution)/shard_map/scale/pallas_call | solution.py:755

commit v6 on v5

--- a/solution.py
+++ b/solution.py
@@ -751,7 +751,7 @@
         ),
         name="solve_all",
     )(source, speed, root_table(length_x, length_z), *sine_table(length_x), *sine_table(length_z))
-    pieces = 16
+    pieces = 32
     return pl.pallas_call(
         scale,
         in_specs=[inside, inside],

time: 52.1 us -> 52.2 us (level)
  no operation moved by 1% of the time
where the time goes in v6:
time: 52.2 us; the launch traced here: 52 us
  Pallas kernels  52 us (100%)
    pallas_call x1, Pallas kernels, on_device(): pl.pallas_call(functools.partial(solve_all, blocks, parts), in_specs=[any...  48.4 us
    pallas_call x1, Pallas kernels, on_device(): pl.pallas_call(scale, in_specs=[inside, inside], out_specs=anywhere, out_...  3.67 us

profile of v6, /device:TPU:0, one launch (start us, length us, event | category | flops | bytes accessed | tf_op | source)
XLA Modules:
  0.0 52.0 jit_solution(9521990432492589099)
XLA Ops:
  0.0 48.4 %solve_all.1 = (f32[4,2,256,8,128]{4,3,2,1,0:T(8,128)S(1)}, f32[8,128]{1,0:T(8,128)S(1)}) custom-call(f32[2,256,32,128]{3,2,1,0:T(8,128)} %source_ref.1, f32[256,32,128]{2,1,0:T(8,128)} %speed_ref.1, f32[2,256,256]{2,1,0:T(8,128)} %constant.6.clone.roots_ref, bf16[256,256]{1,0:T(8,128)(2,1)} %constant.7.clone.x_high_ref.z_high_ref, ...), custom_call_target="tpu_custom_call" | custom-call | tf_op jit(solution)/shard_map/solve_all/pallas_call | solution.py:700
  48.4 3.7 %scale.1 = f32[2,256,32,128]{3,2,1,0:T(8,128)} custom-call(f32[8,128]{1,0:T(8,128)S(1)} %get-tuple-element.7.total_ref, f32[4,2,256,8,128]{4,3,2,1,0:T(8,128)S(1)} %get-tuple-element.8.w_ref), custom_call_target="tpu_custom_call" | custom-call | tf_op jit(solution)/shard_map/scale/pallas_call | solution.py:755
